TPU v7x, 32 devices: a whole 2x2x4 slice. The times are simulated.
32 devices in a mesh: groups: 2 (over x), seq: 8 (over z, y), head: 2 (over core).
Axes of the slice: x: 2, y: 2, z: 4, core: 2. Of those that a mesh axis runs over, the one named last changes fastest.
Arguments:
- queries: bfloat16 [2048, 28, 128], P(('groups', 'seq'), 'head'), parts along dimension 0, may hold values from -400 to 400, as said below
- request_image: int32 [2048, 1], P(('groups', 'seq')), parts along dimension 0, may hold values from 0 to 15; in each aligned block of 128 rows (0 to 127, 128 to 255, ...) at most 16 rows name the same one
- image_slot: int32 [32], P('groups'), parts along dimension 0, may hold values from 0 to 15, each once
- image_lengths: int32 [32], P(('groups', 'seq')), parts along dimension 0, may hold values from 640 to 1280
- image_keys: bfloat16 [32, 4, 1280, 128], P(('groups', 'seq'), 'head'), parts along dimension 0, may hold values from -6 to 6
- image_values: bfloat16 [32, 4, 1280, 128], P(('groups', 'seq'), 'head'), parts along dimension 0, may hold values from -6 to 6
- text_keys: bfloat16 [2048, 4, 64, 128], P(('groups', 'seq'), 'head'), parts along dimension 0, may hold values from -6 to 6
- text_values: bfloat16 [2048, 4, 64, 128], P(('groups', 'seq'), 'head'), parts along dimension 0, may hold values from -6 to 6
- text_lengths: int32 [2048], P(('groups', 'seq')), parts along dimension 0, may hold values from 1 to 64
Outputs:
- attention: bfloat16 [2048, 28, 128], P(('groups', 'seq'), 'head'), parts along dimension 0
There are 2 independent parts, one for each index of `groups`. A program takes and returns all parts, laid end to end along the dimension named above; each array names one. Nothing has to cross between parts.
Inputs may be any that keep to these rules, and one draw needn't show every extreme that they name: queries are finite bfloat16 values. `request_image`: the requests of one index of seq name any one image at most 16 times, and in some index of seq some image is named exactly 16 times. `image_slot`: a permutation; the image in storage slot s is held by index s // 2 of seq.
All inputs are finite; a program needn't handle non-finite values.
Results may differ from a plain program's by a relative error of at most 0.0056.
Values may be sent and summed in bfloat16 or wider, within the bound.
A program may use at most 64 MiB of HBM per device.

v0:
```python
import functools
import math

import jax
import jax.numpy as jnp
from jax import lax
from jax.experimental import pallas as pl
from jax.experimental.pallas import tpu as pltpu
from jax.sharding import PartitionSpec as P

NEGATIVE = -1e30
LOG2E = math.log2(math.e)
LN2 = math.log(2.0)
MESH = pl.DeviceIdType.MESH
BLOCK = 16
LANES = 16
SPLIT = 3
FIRST = 1


def partner(me, step, devices):
    if devices & (devices - 1):
        return lax.rem(step + devices - me, devices)
    other = 0
    bit = 1
    while bit < devices:
        mine = lax.rem(me // bit, 2)
        flip = lax.rem(step // bit, 2)
        other = other + bit * (mine + flip - 2 * mine * flip)
        bit *= 2
    return other


def sent(step):
    return step


def taken(step):
    return step


def attend(query, keys, values, mask, factor):
    scores = lax.dot_general(
        query, keys, (((1,), (1,)), ((), ())), preferred_element_type=jnp.float32
    )
    scores = mask(scores * factor)
    highest = jnp.max(scores, axis=-1, keepdims=True)
    weights = jnp.exp2(scores - highest)
    total = jnp.sum(weights, axis=-1, keepdims=True)
    output = jnp.dot(weights.astype(jnp.bfloat16), values, preferred_element_type=jnp.float32)
    return output / total, (highest + jnp.log2(total)) * LN2


def kernel(
    devices,
    held,
    most,
    group,
    slot_ref,
    length_ref,
    image_ref,
    text_length_ref,
    query_ref,
    ikey_hbm,
    ivalue_hbm,
    tkey_hbm,
    tvalue_hbm,
    out_ref,
    ikey,
    ivalue,
    tkey,
    tvalue,
    send,
    recv,
    result,
    back,
    text_out,
    text_lse,
    lengths,
    local_sem,
    send_sem,
    recv_sem,
    result_sem,
    back_sem,
):
    me = lax.axis_index("seq")
    local_heads, rows, head_size = query_ref.shape
    local_kv = ikey.shape[1]
    image_tokens = ikey.shape[2]
    text_tokens = tkey.shape[2]
    images = slot_ref.shape[0]
    slots = images * most
    blocks = rows // BLOCK
    factor = LOG2E / math.sqrt(head_size)

    loads = [
        pltpu.make_async_copy(source, target, local_sem.at[index])
        for index, (source, target) in enumerate(
            ((tkey_hbm, tkey), (tvalue_hbm, tvalue), (ikey_hbm, ikey), (ivalue_hbm, ivalue))
        )
    ]
    for load in loads:
        load.start()

    barrier = pltpu.get_barrier_semaphore()

    @pl.loop(1, devices)
    def _(step):
        pl.semaphore_signal(
            barrier, inc=1, device_id={"seq": partner(me, step, devices)}, device_id_type=MESH
        )

    image = image_ref[...]
    slot = jnp.zeros_like(image)
    for index in range(images):
        slot = jnp.where(image == index, slot_ref[index], slot)
    hits = slot == lax.broadcasted_iota(jnp.int32, (images, rows), 0)
    earlier = lax.broadcasted_iota(jnp.int32, (rows, rows), 0) < lax.broadcasted_iota(
        jnp.int32, (rows, rows), 1
    )
    counts = jnp.dot(
        hits.astype(jnp.float32).astype(jnp.bfloat16),
        earlier.astype(jnp.float32).astype(jnp.bfloat16),
        preferred_element_type=jnp.float32,
    )
    rank = jnp.sum(jnp.where(hits, counts, 0.0), axis=0, keepdims=True)
    target = slot.astype(jnp.float32) * most + rank
    dispatch = (
        lax.broadcasted_iota(jnp.int32, (slots, rows), 0).astype(jnp.float32) == target
    ).astype(jnp.float32).astype(jnp.bfloat16)
    for head in range(local_heads):
        moved = jnp.dot(dispatch, query_ref[head], preferred_element_type=jnp.float32)
        send[:, :, head] = moved.astype(jnp.bfloat16).reshape(devices, held, most, head_size)

    pl.semaphore_wait(barrier, devices - 1)

    def forward(other):
        return pltpu.make_async_remote_copy(
            src_ref=send.at[other],
            dst_ref=recv.at[me],
            send_sem=send_sem.at[other],
            recv_sem=recv_sem.at[me],
            device_id={"seq": other},
            device_id_type=MESH,
        )

    def arriving(other):
        return pltpu.make_async_remote_copy(
            src_ref=send.at[other],
            dst_ref=recv.at[other],
            send_sem=send_sem.at[other],
            recv_sem=recv_sem.at[other],
            device_id={"seq": other},
            device_id_type=MESH,
        )

    def returning(other):
        return pltpu.make_async_remote_copy(
            src_ref=result.at[other],
            dst_ref=back.at[me],
            send_sem=result_sem.at[other],
            recv_sem=back_sem.at[me],
            device_id={"seq": other},
            device_id_type=MESH,
        )

    def returned(other):
        return pltpu.make_async_remote_copy(
            src_ref=result.at[other],
            dst_ref=back.at[other],
            send_sem=result_sem.at[other],
            recv_sem=back_sem.at[other],
            device_id={"seq": other},
            device_id_type=MESH,
        )

    @pl.loop(1, devices)
    def _(step):
        forward(partner(me, sent(step), devices)).start()

    lengths[...] = jnp.broadcast_to(
        text_length_ref[...].astype(jnp.float32), (rows, rows)
    ).T

    def place(lse, count):
        lane = lax.broadcasted_iota(jnp.int32, (count, head_size), 1)
        plane = jnp.zeros((count, head_size), jnp.float32)
        for head in range(local_heads):
            plane = jnp.where(lane == head, lse[head], plane)
        return plane

    loads[0].wait()
    loads[1].wait()

    def text(block):
        first = block * BLOCK
        first = first if isinstance(first, int) else pl.multiple_of(first, BLOCK)
        window = pl.ds(first, BLOCK)
        token = lax.broadcasted_iota(jnp.int32, (BLOCK, BLOCK * text_tokens), 1)
        offset = (
            token - text_tokens * lax.broadcasted_iota(jnp.int32, token.shape, 0)
        ).astype(jnp.float32)
        valid = (offset >= 0.0) & (offset < lengths[window, 0:1])
        bias = jnp.where(valid, 0.0, NEGATIVE)
        lses = []
        for kv in range(local_kv):
            query = query_ref[kv * group : (kv + 1) * group, window, :]
            query = query.reshape(group * BLOCK, head_size)
            keys = tkey[window, kv].reshape(BLOCK * text_tokens, head_size)
            values = tvalue[window, kv].reshape(BLOCK * text_tokens, head_size)

            def mask(scores):
                scores = scores.reshape(group, BLOCK, BLOCK * text_tokens) + bias[None]
                return scores.reshape(group * BLOCK, BLOCK * text_tokens)

            output, lse = attend(query, keys, values, mask, factor)
            text_out[kv * group : (kv + 1) * group, window, :] = output.reshape(
                group, BLOCK, head_size
            )
            lses += [lse[head * BLOCK : (head + 1) * BLOCK] for head in range(group)]
        text_lse[window, :] = place(lses, BLOCK)

    loads[2].wait()
    loads[3].wait()
    token = lax.broadcasted_iota(jnp.int32, (1, image_tokens), 1)
    biases = [jnp.where(token < length_ref[index], 0.0, NEGATIVE) for index in range(held)]

    def process(source, target):
        packed = jnp.zeros((most, head_size), jnp.float32)
        for index in range(held):
            lses = []
            for kv in range(local_kv):
                query = source[index, kv * group : (kv + 1) * group]
                query = query.reshape(group * most, head_size)
                output, lse = attend(
                    query,
                    ikey[index, kv],
                    ivalue[index, kv],
                    lambda scores: scores + biases[index],
                    factor,
                )
                start = index * local_heads + kv * group
                target[start : start + group] = output.astype(
                    jnp.bfloat16
                ).reshape(group, most, head_size)
                lses += [lse[head * most : (head + 1) * most] for head in range(group)]
            plane = place(lses, most)
            high = plane.astype(jnp.bfloat16).astype(jnp.float32)
            rest = plane - high
            middle = rest.astype(jnp.bfloat16).astype(jnp.float32)
            low = rest - middle
            for part, piece in enumerate((high, middle, low)):
                shift = LANES * (SPLIT * index + part)
                packed = packed + (pltpu.roll(piece, shift, 1) if shift else piece)
        target[held * local_heads] = packed.astype(jnp.bfloat16)

    for block in range(FIRST):
        text(block)
    process(send.at[me], back.at[me])

    @pl.loop(1, devices)
    def _(step):
        other = partner(me, taken(step), devices)

        @pl.when(step + (FIRST - 1) < blocks)
        def _():
            text(step + (FIRST - 1))

        arriving(other).wait_recv()
        process(recv.at[other], result.at[other])
        returning(other).start()

    for block in range(devices + FIRST - 1, blocks):
        text(block)

    sought = jnp.broadcast_to(target, (rows, rows)).T
    lane = lax.broadcasted_iota(jnp.int32, (rows, rows), 1).astype(jnp.float32)
    combine = jnp.concatenate(
        [
            (sought == lane + float(start)).astype(jnp.float32).astype(jnp.bfloat16)
            for start in range(0, slots, rows)
        ],
        axis=1,
    )

    @pl.loop(1, devices)
    def _(step):
        other = partner(me, taken(step), devices)
        forward(other).wait_send()
        returning(other).wait_send()
        returned(other).wait_recv()

    planes = back[:, held * local_heads].reshape(devices, 1, most, head_size)
    spread = jnp.broadcast_to(planes, (devices, held, most, head_size)).reshape(slots, head_size)
    at_lane = lax.broadcasted_iota(jnp.int32, (1, 1, 1, head_size), 3)
    at_held = lax.broadcasted_iota(jnp.int32, (1, held, 1, 1), 1)
    low_lane = at_held * (SPLIT * LANES)
    own_lanes = (at_lane >= low_lane) & (at_lane < low_lane + SPLIT * LANES)
    own_lanes = jnp.broadcast_to(
        own_lanes.astype(jnp.float32), (devices, held, most, head_size)
    ).reshape(slots, head_size).astype(jnp.bfloat16)
    parts = jnp.dot(combine, spread * own_lanes, preferred_element_type=jnp.float32)
    image_lse = parts
    for piece in range(1, SPLIT * held):
        image_lse = image_lse + pltpu.roll(parts, head_size - LANES * piece, 1)
    own_lse = text_lse[...]
    upper = jnp.maximum(image_lse, own_lse)
    image_weight = jnp.exp(image_lse - upper)
    text_weight = jnp.exp(own_lse - upper)
    whole = image_weight + text_weight
    image_weight = image_weight / whole
    text_weight = text_weight / whole
    def gathered(head):
        pieces = [back[:, index * local_heads + head] for index in range(held)]
        return jnp.stack(pieces, axis=1).reshape(slots, head_size)

    for head in range(local_heads):
        image_part = jnp.dot(
            combine,
            gathered(head),
            preferred_element_type=jnp.float32,
        )
        merged = (
            image_weight[:, head : head + 1] * image_part
            + text_weight[:, head : head + 1] * text_out[head]
        )
        out_ref[head] = merged.astype(jnp.bfloat16)


def on_device(
    queries,
    request_image,
    image_slot,
    image_lengths,
    image_keys,
    image_values,
    text_keys,
    text_values,
    text_lengths,
):
    rows, local_heads, head_size = queries.shape
    held, local_kv, image_tokens, _ = image_keys.shape
    text_tokens = text_keys.shape[2]
    group = local_heads // local_kv
    images = image_slot.shape[0]
    devices = lax.axis_size("seq")
    most = -(-max(2, 2 * rows // images) // BLOCK) * BLOCK
    smem = pl.BlockSpec(memory_space=pltpu.SMEM)
    vmem = pl.BlockSpec(memory_space=pltpu.VMEM)
    hbm = pl.BlockSpec(memory_space=pl.ANY)
    moved = pl.pallas_call(
        functools.partial(kernel, devices, held, most, group),
        out_shape=jax.ShapeDtypeStruct((local_heads, rows, head_size), jnp.bfloat16),
        in_specs=[smem, smem, vmem, vmem, vmem, hbm, hbm, hbm, hbm],
        out_specs=vmem,
        scratch_shapes=[
            pltpu.VMEM(image_keys.shape, jnp.bfloat16),
            pltpu.VMEM(image_values.shape, jnp.bfloat16),
            pltpu.VMEM(text_keys.shape, jnp.bfloat16),
            pltpu.VMEM(text_values.shape, jnp.bfloat16),
            pltpu.VMEM((devices, held, local_heads, most, head_size), jnp.bfloat16),
            pltpu.VMEM((devices, held, local_heads, most, head_size), jnp.bfloat16),
            pltpu.VMEM((devices, held * local_heads + 1, most, head_size), jnp.bfloat16),
            pltpu.VMEM((devices, held * local_heads + 1, most, head_size), jnp.bfloat16),
            pltpu.VMEM((local_heads, rows, head_size), jnp.float32),
            pltpu.VMEM((rows, head_size), jnp.float32),
            pltpu.VMEM((rows, rows), jnp.float32),
            pltpu.SemaphoreType.DMA((4,)),
            pltpu.SemaphoreType.DMA((devices,)),
            pltpu.SemaphoreType.DMA((devices,)),
            pltpu.SemaphoreType.DMA((devices,)),
            pltpu.SemaphoreType.DMA((devices,)),
        ],
        compiler_params=pltpu.CompilerParams(
            collective_id=0, has_side_effects=True, vmem_limit_bytes=56 * 1024 * 1024
        ),
    )(
        image_slot,
        image_lengths,
        request_image.reshape(1, rows),
        text_lengths.reshape(1, rows),
        jnp.transpose(queries, (1, 0, 2)),
        image_keys,
        image_values,
        text_keys,
        text_values,
    )
    return jnp.transpose(moved, (1, 0, 2))


def solution(mesh):
    in_specs = (
        P(("groups", "seq"), "head", None),
        P(("groups", "seq"), None),
        P("groups"),
        P(("groups", "seq")),
        P(("groups", "seq"), "head", None, None),
        P(("groups", "seq"), "head", None, None),
        P(("groups", "seq"), "head", None, None),
        P(("groups", "seq"), "head", None, None),
        P(("groups", "seq")),
    )
    out_specs = P(("groups", "seq"), "head", None)
    return jax.shard_map(
        on_device, mesh=mesh, in_specs=in_specs, out_specs=out_specs, check_vma=False
    )
```

profile of v0, /device:TPU:8, one launch (start us, length us, event | category | flops | bytes accessed | tf_op | source)
XLA Modules:
  0.0 49.5 jit_solution(14241227023063405864)
XLA Ops:
  0.0 47.7 %shard_map.91 = bf16[14,128,128]{2,1,0:T(8,128)(2,1)} custom-call(s32[16]{0:T(128)} %slot_ref.1, s32[2]{0:T(128)} %length_ref.1, s32[1,128]{1,0:T(1,128)} %bitcast.6, s32[1,128]{1,0:T(1,128)} %bitcast.7, bf16[14,128,128]{2,1,0:T(8,128)(2,1)} %bitcast.5, bf16[2,2,1280,128]{3,2,1,0:T(8,128)(2,1)} %ikey_hbm.1, bf16[2,2,1280,128]{3,2,1,0:T(8,128)(2,1)} %ivalue_hbm.1, ...), custom_call_target="tpu_custom_call" | custom-call | tf_op jit(solution)/shard_map/pallas_call | solution.py:351
  47.7 1.8 %copy.11 = bf16[128,14,128]{2,0,1:T(8,128)(2,1)} copy(bf16[128,14,128]{2,0,1:T(8,128)(2,1)} %bitcast.4) | data formatting | bytes 917504
where the time goes:
time: 49.7 us; the launch traced here: 49.5 us
  Pallas kernels  47.7 us (96%)
  local copies, waits for them, and re-layouts  1.82 us (4%)
    pallas_call x1, Pallas kernels, on_device(): pl.pallas_call(functools.partial(kernel, devices, held, most, group), out...  47.7 us
    unnamed x1, local copies, waits for them, and re-layouts  1.82 us

commit v1 on v0

--- a/solution.py
+++ b/solution.py
@@ -16,11 +16,10 @@
 LANES = 16
 SPLIT = 3
 FIRST = 1
+LIMIT = 48 * 1024 * 1024
 
 
 def partner(me, step, devices):
-    if devices & (devices - 1):
-        return lax.rem(step + devices - me, devices)
     other = 0
     bit = 1
     while bit < devices:
@@ -31,14 +30,6 @@
     return other
 
 
-def sent(step):
-    return step
-
-
-def taken(step):
-    return step
-
-
 def attend(query, keys, values, mask, factor):
     scores = lax.dot_general(
         query, keys, (((1,), (1,)), ((), ())), preferred_element_type=jnp.float32
@@ -56,16 +47,21 @@
     held,
     most,
     group,
+    slot_hbm,
+    length_hbm,
+    image_hbm,
+    text_length_hbm,
+    query_hbm,
+    ikey_hbm,
+    ivalue_hbm,
+    tkey_hbm,
+    tvalue_hbm,
+    out_ref,
     slot_ref,
     length_ref,
     image_ref,
     text_length_ref,
     query_ref,
-    ikey_hbm,
-    ivalue_hbm,
-    tkey_hbm,
-    tvalue_hbm,
-    out_ref,
     ikey,
     ivalue,
     tkey,
@@ -93,15 +89,6 @@
     blocks = rows // BLOCK
     factor = LOG2E / math.sqrt(head_size)
 
-    loads = [
-        pltpu.make_async_copy(source, target, local_sem.at[index])
-        for index, (source, target) in enumerate(
-            ((tkey_hbm, tkey), (tvalue_hbm, tvalue), (ikey_hbm, ikey), (ivalue_hbm, ivalue))
-        )
-    ]
-    for load in loads:
-        load.start()
-
     barrier = pltpu.get_barrier_semaphore()
 
     @pl.loop(1, devices)
@@ -110,10 +97,34 @@
             barrier, inc=1, device_id={"seq": partner(me, step, devices)}, device_id_type=MESH
         )
 
+    copies = [
+        pltpu.make_async_copy(source, target, local_sem.at[index])
+        for index, (source, target) in enumerate(
+            (
+                (query_hbm, query_ref),
+                (slot_hbm, slot_ref),
+                (image_hbm, image_ref),
+                (length_hbm, length_ref),
+                (text_length_hbm, text_length_ref),
+                (tkey_hbm, tkey),
+                (tvalue_hbm, tvalue),
+                (ikey_hbm, ikey),
+                (ivalue_hbm, ivalue),
+            )
+        )
+    ]
+    for copy in copies:
+        copy.start()
+    loads = copies[5:]
+
+    copies[1].wait()
+    copies[2].wait()
     image = image_ref[...]
     slot = jnp.zeros_like(image)
     for index in range(images):
-        slot = jnp.where(image == index, slot_ref[index], slot)
+        place = slot_ref[index]
+        place = partner(me, place // held, devices) * held + lax.rem(place, held)
+        slot = jnp.where(image == index, place, slot)
     hits = slot == lax.broadcasted_iota(jnp.int32, (images, rows), 0)
     earlier = lax.broadcasted_iota(jnp.int32, (rows, rows), 0) < lax.broadcasted_iota(
         jnp.int32, (rows, rows), 1
@@ -128,56 +139,39 @@
     dispatch = (
         lax.broadcasted_iota(jnp.int32, (slots, rows), 0).astype(jnp.float32) == target
     ).astype(jnp.float32).astype(jnp.bfloat16)
+    copies[0].wait()
     for head in range(local_heads):
         moved = jnp.dot(dispatch, query_ref[head], preferred_element_type=jnp.float32)
         send[:, :, head] = moved.astype(jnp.bfloat16).reshape(devices, held, most, head_size)
 
     pl.semaphore_wait(barrier, devices - 1)
 
-    def forward(other):
+    def forward(step):
         return pltpu.make_async_remote_copy(
-            src_ref=send.at[other],
-            dst_ref=recv.at[me],
-            send_sem=send_sem.at[other],
-            recv_sem=recv_sem.at[me],
-            device_id={"seq": other},
+            src_ref=send.at[step],
+            dst_ref=recv.at[step],
+            send_sem=send_sem.at[step],
+            recv_sem=recv_sem.at[step],
+            device_id={"seq": partner(me, step, devices)},
             device_id_type=MESH,
         )
 
-    def arriving(other):
+    def returning(step):
         return pltpu.make_async_remote_copy(
-            src_ref=send.at[other],
-            dst_ref=recv.at[other],
-            send_sem=send_sem.at[other],
-            recv_sem=recv_sem.at[other],
-            device_id={"seq": other},
-            device_id_type=MESH,
-        )
-
-    def returning(other):
-        return pltpu.make_async_remote_copy(
-            src_ref=result.at[other],
-            dst_ref=back.at[me],
-            send_sem=result_sem.at[other],
-            recv_sem=back_sem.at[me],
-            device_id={"seq": other},
-            device_id_type=MESH,
-        )
-
-    def returned(other):
-        return pltpu.make_async_remote_copy(
-            src_ref=result.at[other],
-            dst_ref=back.at[other],
-            send_sem=result_sem.at[other],
-            recv_sem=back_sem.at[other],
-            device_id={"seq": other},
+            src_ref=result.at[step],
+            dst_ref=back.at[step],
+            send_sem=result_sem.at[step],
+            recv_sem=back_sem.at[step],
+            device_id={"seq": partner(me, step, devices)},
             device_id_type=MESH,
         )
 
     @pl.loop(1, devices)
     def _(step):
-        forward(partner(me, sent(step), devices)).start()
-
+        forward(step).start()
+
+    copies[3].wait()
+    copies[4].wait()
     lengths[...] = jnp.broadcast_to(
         text_length_ref[...].astype(jnp.float32), (rows, rows)
     ).T
@@ -256,19 +250,17 @@
 
     for block in range(FIRST):
         text(block)
-    process(send.at[me], back.at[me])
+    process(send.at[0], back.at[0])
 
     @pl.loop(1, devices)
     def _(step):
-        other = partner(me, taken(step), devices)
-
         @pl.when(step + (FIRST - 1) < blocks)
         def _():
             text(step + (FIRST - 1))
 
-        arriving(other).wait_recv()
-        process(recv.at[other], result.at[other])
-        returning(other).start()
+        forward(step).wait_recv()
+        process(recv.at[step], result.at[step])
+        returning(step).start()
 
     for block in range(devices + FIRST - 1, blocks):
         text(block)
@@ -285,10 +277,9 @@
 
     @pl.loop(1, devices)
     def _(step):
-        other = partner(me, taken(step), devices)
-        forward(other).wait_send()
-        returning(other).wait_send()
-        returned(other).wait_recv()
+        forward(step).wait_send()
+        returning(step).wait_send()
+        returning(step).wait_recv()
 
     planes = back[:, held * local_heads].reshape(devices, 1, most, head_size)
     spread = jnp.broadcast_to(planes, (devices, held, most, head_size)).reshape(slots, head_size)
@@ -345,15 +336,18 @@
     images = image_slot.shape[0]
     devices = lax.axis_size("seq")
     most = -(-max(2, 2 * rows // images) // BLOCK) * BLOCK
-    smem = pl.BlockSpec(memory_space=pltpu.SMEM)
-    vmem = pl.BlockSpec(memory_space=pltpu.VMEM)
-    hbm = pl.BlockSpec(memory_space=pl.ANY)
+    hbm = pl.BlockSpec(memory_space=pltpu.HBM)
     moved = pl.pallas_call(
         functools.partial(kernel, devices, held, most, group),
-        out_shape=jax.ShapeDtypeStruct((local_heads, rows, head_size), jnp.bfloat16),
-        in_specs=[smem, smem, vmem, vmem, vmem, hbm, hbm, hbm, hbm],
-        out_specs=vmem,
+        out_shape=pltpu.VMEM((local_heads, rows, head_size), jnp.bfloat16),
+        in_specs=[hbm] * 9,
+        out_specs=pl.BlockSpec(memory_space=pltpu.VMEM),
         scratch_shapes=[
+            pltpu.SMEM(image_slot.shape, jnp.int32),
+            pltpu.SMEM(image_lengths.shape, jnp.int32),
+            pltpu.VMEM((1, rows), jnp.int32),
+            pltpu.VMEM((1, rows), jnp.int32),
+            pltpu.VMEM((local_heads, rows, head_size), jnp.bfloat16),
             pltpu.VMEM(image_keys.shape, jnp.bfloat16),
             pltpu.VMEM(image_values.shape, jnp.bfloat16),
             pltpu.VMEM(text_keys.shape, jnp.bfloat16),
@@ -365,25 +359,30 @@
             pltpu.VMEM((local_heads, rows, head_size), jnp.float32),
             pltpu.VMEM((rows, head_size), jnp.float32),
             pltpu.VMEM((rows, rows), jnp.float32),
-            pltpu.SemaphoreType.DMA((4,)),
+            pltpu.SemaphoreType.DMA((9,)),
             pltpu.SemaphoreType.DMA((devices,)),
             pltpu.SemaphoreType.DMA((devices,)),
             pltpu.SemaphoreType.DMA((devices,)),
             pltpu.SemaphoreType.DMA((devices,)),
         ],
         compiler_params=pltpu.CompilerParams(
-            collective_id=0, has_side_effects=True, vmem_limit_bytes=56 * 1024 * 1024
+            collective_id=0, has_side_effects=True, vmem_limit_bytes=LIMIT
         ),
     )(
-        image_slot,
-        image_lengths,
-        request_image.reshape(1, rows),
-        text_lengths.reshape(1, rows),
-        jnp.transpose(queries, (1, 0, 2)),
-        image_keys,
-        image_values,
-        text_keys,
-        text_values,
+        *(
+            pltpu.with_memory_space_constraint(operand, pltpu.HBM)
+            for operand in (
+                image_slot,
+                image_lengths,
+                request_image.reshape(1, rows),
+                text_lengths.reshape(1, rows),
+                jnp.transpose(queries, (1, 0, 2)),
+                image_keys,
+                image_values,
+                text_keys,
+                text_values,
+            )
+        )
     )
     return jnp.transpose(moved, (1, 0, 2))
 

time: 49.7 us -> 47.2 us (0.950)
  the two profiles are of different devices: /device:TPU:8 before, /device:TPU:10 now
where the time goes in v1:
time: 47.2 us; the launch traced here: 47 us
  Pallas kernels  46.2 us (98%)
  local copies, waits for them, and re-layouts  0.77 us (2%)
    pallas_call x1, Pallas kernels, on_device(): pl.pallas_call(functools.partial(kernel, devices, held, most, group), out...  46.2 us

profile of v1, /device:TPU:10, one launch (start us, length us, event | category | flops | bytes accessed | tf_op | source)
XLA Modules:
  0.0 47.0 jit_solution(16021530571041613421)
XLA Ops:
  0.0 46.2 %shard_map.91 = bf16[14,128,128]{2,1,0:T(8,128)(2,1)S(1)} custom-call(s32[16]{0:T(128)} %slot_hbm.1, s32[2]{0:T(128)} %length_hbm.1, s32[1,128]{1,0:T(1,128)} %bitcast.6, s32[1,128]{1,0:T(1,128)} %bitcast.7, bf16[14,128,128]{2,1,0:T(8,128)(2,1)} %bitcast.5, bf16[2,2,1280,128]{3,2,1,0:T(8,128)(2,1)} %ikey_hbm.1, bf16[2,2,1280,128]{3,2,1,0:T(8,128)(2,1)} %ivalue_hbm.1, ...), custom_call_target="tpu_custom_call" | custom-call | tf_op jit(solution)/shard_map/pallas_call | solution.py:340
  46.2 0.8 %copy.11 = bf16[128,14,128]{2,0,1:T(8,128)(2,1)} copy(bf16[128,14,128]{2,0,1:T(8,128)(2,1)S(1)} %bitcast.4) | data formatting | bytes 917504

commit v2 on v1

--- a/solution.py
+++ b/solution.py
@@ -318,6 +318,550 @@
         out_ref[head] = merged.astype(jnp.bfloat16)
 
 
+def spread_planes(planes, held):
+    units, _, head_size = planes.shape
+    planes = planes.reshape(units, 1, BLOCK, head_size)
+    spread = jnp.broadcast_to(planes, (units, held, BLOCK, head_size))
+    at_lane = lax.broadcasted_iota(jnp.int32, (1, 1, 1, head_size), 3)
+    at_held = lax.broadcasted_iota(jnp.int32, (1, held, 1, 1), 1)
+    low_lane = at_held * (SPLIT * LANES)
+    own_lanes = (at_lane >= low_lane) & (at_lane < low_lane + SPLIT * LANES)
+    own_lanes = jnp.broadcast_to(own_lanes.astype(jnp.float32), spread.shape)
+    own_lanes = own_lanes.reshape(-1, head_size).astype(jnp.bfloat16)
+    return spread.reshape(-1, head_size) * own_lanes
+
+
+def place(lse, count, head_size):
+    lane = lax.broadcasted_iota(jnp.int32, (count, head_size), 1)
+    plane = jnp.zeros((count, head_size), jnp.float32)
+    for head, column in enumerate(lse):
+        plane = jnp.where(lane == head, column, plane)
+    return plane
+
+
+def one_hot(condition):
+    return condition.astype(jnp.float32).astype(jnp.bfloat16)
+
+
+def cross_lanes(left, right):
+    return lax.dot_general(
+        left, right, (((1,), (1,)), ((), ())), preferred_element_type=jnp.float32
+    )
+
+
+LOCAL = 4
+OWN, NEAR, OVER, BASE = 0, (0, 1, 2, 7), (3, 5), (4, 6)
+UNITS = 8
+BLOCKS = (*NEAR, *BASE)
+EARLY = 3
+
+
+def fast_kernel(
+    devices,
+    replicas,
+    held,
+    group,
+    spare,
+    slot_hbm,
+    length_hbm,
+    image_hbm,
+    text_length_hbm,
+    query_hbm,
+    ikey_hbm,
+    ivalue_hbm,
+    tkey_hbm,
+    tvalue_hbm,
+    out_ref,
+    flag_ref,
+    slot_ref,
+    length_ref,
+    image_ref,
+    text_length_ref,
+    query_ref,
+    ikey,
+    ivalue,
+    tkey,
+    tvalue,
+    send,
+    recv,
+    result,
+    back,
+    fan,
+    ret,
+    bundle_send,
+    bundle_recv,
+    bundle_result,
+    bundle_back,
+    metas,
+    group_send,
+    group_recv,
+    text_out,
+    text_lse,
+    lengths,
+    local_sem,
+    send_sem,
+    recv_sem,
+    result_sem,
+    back_sem,
+    fan_sem,
+    fan_recv_sem,
+    ret_sem,
+    ret_recv_sem,
+    bundle_sem,
+    meta_sem,
+    meta_recv_sem,
+    group_sem,
+    group_recv_sem,
+):
+    me = lax.axis_index("seq")
+    replica = lax.axis_index("groups")
+    local_heads, rows, head_size = query_ref.shape
+    local_kv = ikey.shape[1]
+    image_tokens = ikey.shape[2]
+    text_tokens = tkey.shape[2]
+    images = slot_ref.shape[0]
+    half = BLOCK // 2
+    near = LOCAL * held
+    text_blocks = rows // BLOCK
+    factor = LOG2E / math.sqrt(head_size)
+
+    barrier = pltpu.get_barrier_semaphore()
+
+    @pl.loop(1, devices)
+    def _(step):
+        pl.semaphore_signal(
+            barrier, inc=1, device_id={"seq": partner(me, step, devices)}, device_id_type=MESH
+        )
+
+    for turn in range(1, replicas):
+        pl.semaphore_signal(
+            barrier,
+            inc=1,
+            device_id={"groups": lax.rem(replica + turn, replicas)},
+            device_id_type=MESH,
+        )
+
+    copies = [
+        pltpu.make_async_copy(source, target, local_sem.at[index])
+        for index, (source, target) in enumerate(
+            (
+                (query_hbm, query_ref),
+                (slot_hbm, slot_ref),
+                (image_hbm, image_ref),
+                (length_hbm, length_ref),
+                (text_length_hbm, text_length_ref),
+                (tkey_hbm, tkey),
+                (tvalue_hbm, tvalue),
+                (ikey_hbm, ikey),
+                (ivalue_hbm, ivalue),
+            )
+        )
+    ]
+    for copy in copies:
+        copy.start()
+    loads = copies[5:]
+
+    copies[1].wait()
+    copies[2].wait()
+
+    earlier = one_hot(
+        lax.broadcasted_iota(jnp.int32, (rows, rows), 0)
+        < lax.broadcasted_iota(jnp.int32, (rows, rows), 1)
+    )
+
+    def route(image, origin):
+        step = jnp.zeros(image.shape, jnp.float32)
+        index = jnp.zeros(image.shape, jnp.float32)
+        spot = jnp.zeros(image.shape, jnp.int32)
+        for name in range(images):
+            slot = slot_ref[name]
+            owner = partner(origin, slot // held, devices)
+            which = lax.rem(slot, held)
+            step = jnp.where(image == name, owner.astype(jnp.float32), step)
+            index = jnp.where(image == name, which.astype(jnp.float32), index)
+            spot = jnp.where(image == name, slot, spot)
+        hits = spot == lax.broadcasted_iota(jnp.int32, (images, rows), 0)
+        counts = jnp.dot(one_hot(hits), earlier, preferred_element_type=jnp.float32)
+        rank = jnp.sum(jnp.where(hits, counts, 0.0), axis=0, keepdims=True)
+        over = (step >= LOCAL) & (rank >= half)
+        over = jnp.where(over, 1.0, 0.0)
+        order = jnp.dot(
+            jnp.broadcast_to(over, (BLOCK, rows)).astype(jnp.bfloat16),
+            earlier,
+            preferred_element_type=jnp.float32,
+        )[0:1]
+        return step, index, rank, over > 0.0, order
+
+    def paired(step, index, rank):
+        pair = jnp.where(step >= 2.0, 1.0, 0.0)
+        parity = step - 2.0 * pair
+        return (pair * held + index) * BLOCK + parity * half + rank
+
+    step, index, rank, over, order = route(image_ref[...], me)
+    target = jnp.where(
+        step < LOCAL,
+        (step * held + index) * BLOCK + rank,
+        jnp.where(
+            over,
+            (LOCAL + 2.0) * held * BLOCK + order,
+            LOCAL * held * BLOCK + paired(step - LOCAL, index, rank),
+        ),
+    )
+    places = (LOCAL + 2) * held * BLOCK + spare
+    dispatch = one_hot(
+        lax.broadcasted_iota(jnp.int32, (places, rows), 0).astype(jnp.float32) == target
+    )
+    copies[0].wait()
+    for head in range(local_heads):
+        moved = jnp.dot(dispatch, query_ref[head], preferred_element_type=jnp.float32)
+        moved = moved.astype(jnp.bfloat16)
+        blocks = moved[: (LOCAL + 2) * held * BLOCK].reshape(-1, held, BLOCK, head_size)
+        recv[OWN, :, head] = blocks[0]
+        send[:, :, head] = blocks[1:]
+        bundle_send[head] = moved[(LOCAL + 2) * held * BLOCK :]
+
+    pl.semaphore_wait(barrier, devices - 1 + replicas - 1)
+
+    def remote(source, sink, source_sem, sink_sem, step):
+        return pltpu.make_async_remote_copy(
+            src_ref=source,
+            dst_ref=sink,
+            send_sem=source_sem,
+            recv_sem=sink_sem,
+            device_id={"seq": partner(me, step, devices)},
+            device_id_type=MESH,
+        )
+
+    def meta(step):
+        return remote(image_ref, metas.at[step], meta_sem.at[step], meta_recv_sem.at[step], step)
+
+    def bundle_out():
+        return remote(bundle_send, bundle_recv, bundle_sem.at[0], bundle_sem.at[1], LOCAL)
+
+    def bundle_home():
+        return remote(bundle_result, bundle_back, bundle_sem.at[2], bundle_sem.at[3], LOCAL)
+
+    def part(parity):
+        return pl.ds(parity * half, half)
+
+    def forward(step):
+        if step < LOCAL:
+            source, sink = send.at[step - 1], recv.at[NEAR[step]]
+        else:
+            pair, parity = divmod(step - LOCAL, 2)
+            source = send.at[LOCAL - 1 + pair, :, :, part(parity)]
+            sink = recv.at[BASE[pair], :, :, part(parity)]
+        return remote(source, sink, send_sem.at[step], recv_sem.at[step], step)
+
+    def returning(step):
+        if step < LOCAL:
+            source, sink = result.at[NEAR[step]], back.at[NEAR[step]]
+        else:
+            pair, parity = divmod(step - LOCAL, 2)
+            source = result.at[BASE[pair], :, part(parity)]
+            sink = back.at[BASE[pair], :, part(parity)]
+        return remote(source, sink, result_sem.at[step], back_sem.at[step], step)
+
+    def fan_out(step):
+        pair, parity = divmod(step, 2)
+        source = fan.at[pair, :, :, part(parity)]
+        sink = recv.at[OVER[pair], :, :, part(parity)]
+        return remote(source, sink, fan_sem.at[step], fan_recv_sem.at[step], step)
+
+    def fan_home(step):
+        pair, parity = divmod(step, 2)
+        source = result.at[OVER[pair], :, part(parity)]
+        sink = ret.at[pair, :, part(parity)]
+        return remote(source, sink, ret_sem.at[step], ret_recv_sem.at[step], step)
+
+    @pl.loop(1, devices)
+    def _(step):
+        meta(step).start()
+
+    bundle_out().start()
+    for step in range(1, devices):
+        forward(step).start()
+
+    copies[3].wait()
+    copies[4].wait()
+    lengths[...] = jnp.broadcast_to(
+        text_length_ref[...].astype(jnp.float32), (rows, rows)
+    ).T
+
+    loads[0].wait()
+    loads[1].wait()
+
+    def text(block):
+        window = pl.ds(pl.multiple_of(block * BLOCK, BLOCK), BLOCK)
+        token = lax.broadcasted_iota(jnp.int32, (BLOCK, BLOCK * text_tokens), 1)
+        offset = (
+            token - text_tokens * lax.broadcasted_iota(jnp.int32, token.shape, 0)
+        ).astype(jnp.float32)
+        valid = (offset >= 0.0) & (offset < lengths[window, 0:1])
+        bias = jnp.where(valid, 0.0, NEGATIVE)
+        lses = []
+        for kv in range(local_kv):
+            query = query_ref[kv * group : (kv + 1) * group, window, :]
+            query = query.reshape(group * BLOCK, head_size)
+            keys = tkey[window, kv].reshape(BLOCK * text_tokens, head_size)
+            values = tvalue[window, kv].reshape(BLOCK * text_tokens, head_size)
+
+            def mask(scores):
+                scores = scores.reshape(group, BLOCK, BLOCK * text_tokens) + bias[None]
+                return scores.reshape(group * BLOCK, BLOCK * text_tokens)
+
+            output, lse = attend(query, keys, values, mask, factor)
+            text_out[kv * group : (kv + 1) * group, window, :] = output.reshape(
+                group, BLOCK, head_size
+            )
+            lses += [lse[head * BLOCK : (head + 1) * BLOCK] for head in range(group)]
+        text_lse[window, :] = place(lses, BLOCK, head_size)
+
+    @pl.loop(0, EARLY)
+    def _(block):
+        text(block)
+
+    loads[2].wait()
+    loads[3].wait()
+    token = lax.broadcasted_iota(jnp.int32, (1, image_tokens), 1)
+    biases = [jnp.where(token < length_ref[index], 0.0, NEGATIVE) for index in range(held)]
+
+    def process(source, sink):
+        packed = jnp.zeros((BLOCK, head_size), jnp.float32)
+        for index in range(held):
+            lses = []
+            for kv in range(local_kv):
+                query = source[index, kv * group : (kv + 1) * group]
+                query = query.reshape(group * BLOCK, head_size)
+                output, lse = attend(
+                    query,
+                    ikey[index, kv],
+                    ivalue[index, kv],
+                    lambda scores: scores + biases[index],
+                    factor,
+                )
+                start = index * local_heads + kv * group
+                sink[start : start + group] = output.astype(jnp.bfloat16).reshape(
+                    group, BLOCK, head_size
+                )
+                lses += [lse[head * BLOCK : (head + 1) * BLOCK] for head in range(group)]
+            plane = place(lses, BLOCK, head_size)
+            high = plane.astype(jnp.bfloat16).astype(jnp.float32)
+            rest = plane - high
+            middle = rest.astype(jnp.bfloat16).astype(jnp.float32)
+            low = rest - middle
+            for number, piece in enumerate((high, middle, low)):
+                shift = LANES * (SPLIT * index + number)
+                packed = packed + (pltpu.roll(piece, shift, 1) if shift else piece)
+        sink[held * local_heads] = packed.astype(jnp.bfloat16)
+
+    def relay_places():
+        other = partner(me, LOCAL, devices)
+        step, index, rank, over, order = route(metas[LOCAL], other)
+        spot = jnp.where(over, paired(step - LOCAL, index, rank - half), -1.0)
+        order = jnp.where(over, order, -1.0)
+        spots = LOCAL * held * half
+        spot = one_hot(
+            lax.broadcasted_iota(jnp.int32, (spots, rows), 0).astype(jnp.float32) == spot
+        )
+        order = one_hot(
+            lax.broadcasted_iota(jnp.int32, (spare, rows), 0).astype(jnp.float32) == order
+        )
+        return spot, order
+
+    def relay():
+        bundle_out().wait_recv()
+        spot, order = relay_places()
+        scatter = cross_lanes(spot, order).astype(jnp.bfloat16)
+        for head in range(local_heads):
+            moved = jnp.dot(scatter, bundle_recv[head], preferred_element_type=jnp.float32)
+            moved = moved.astype(jnp.bfloat16).reshape(2, held, BLOCK, head_size)
+            fan[:, :, head] = moved
+            recv[OVER[0], :, head, 0:half] = moved[0, :, 0:half]
+        for step in range(1, LOCAL):
+            fan_out(step).start()
+
+    def collect():
+        for step in range(1, LOCAL):
+            fan_home(step).wait_recv()
+        spot, order = relay_places()
+        gather = cross_lanes(order, spot).astype(jnp.bfloat16)
+        upper = lax.broadcasted_iota(jnp.int32, (BLOCK, head_size), 0) < half
+
+        def tile(pair, number):
+            if pair:
+                return ret[pair, number]
+            own = result[OVER[0], number].astype(jnp.float32)
+            return jnp.where(upper, own, ret[0, number].astype(jnp.float32)).astype(jnp.bfloat16)
+
+        for head in range(local_heads):
+            pieces = [
+                tile(pair, which * local_heads + head) for pair in range(2) for which in range(held)
+            ]
+            moved = jnp.dot(
+                gather, jnp.concatenate(pieces, axis=0), preferred_element_type=jnp.float32
+            )
+            bundle_result[head] = moved.astype(jnp.bfloat16)
+        planes = jnp.stack([tile(pair, held * local_heads) for pair in range(2)], axis=0)
+        moved = jnp.dot(gather, spread_planes(planes, held), preferred_element_type=jnp.float32)
+        bundle_result[local_heads] = moved.astype(jnp.bfloat16)
+        bundle_home().start()
+
+    def judge():
+        @pl.loop(1, devices)
+        def _(step):
+            meta(step).wait_recv()
+
+        mine = lax.rem(me // LOCAL, 2)
+        named = jnp.concatenate(
+            [image_ref[...]] + [metas[step] for step in range(1, devices)], axis=0
+        )
+        side = lax.broadcasted_iota(jnp.int32, (devices, 1), 0) >= LOCAL
+        total = jnp.zeros((devices, 1), jnp.float32)
+        for name in range(images):
+            there = lax.rem(slot_ref[name] // held // LOCAL, 2)
+            apart = (mine + there - 2 * mine * there).astype(jnp.float32)
+            count = jnp.sum(jnp.where(named == name, 1.0, 0.0), axis=1, keepdims=True)
+            excess = jnp.maximum(count - half, 0.0)
+            total = total + excess * jnp.where(side, 1.0 - apart, apart)
+        full = jnp.where(total > spare, 1.0, 0.0)
+        full = jnp.max(full, axis=0, keepdims=True)
+        group_send[...] = jnp.broadcast_to(full, (1, rows)).astype(jnp.int32)
+
+    def tell(turn):
+        return pltpu.make_async_remote_copy(
+            src_ref=group_send,
+            dst_ref=group_recv.at[turn - 1],
+            send_sem=group_sem.at[turn - 1],
+            recv_sem=group_recv_sem.at[turn - 1],
+            device_id={"groups": lax.rem(replica + turn, replicas)},
+            device_id_type=MESH,
+        )
+
+    judge()
+    for turn in range(1, replicas):
+        tell(turn).start()
+
+    @pl.loop(0, UNITS)
+    def _(unit):
+        for step in range(1, LOCAL):
+            @pl.when(unit == NEAR[step])
+            def _():
+                forward(step).wait_recv()
+
+        for pair in range(2):
+            @pl.when(unit == OVER[pair])
+            def _():
+                for step in range(max(1, 2 * pair), 2 * pair + 2):
+                    fan_out(step).wait_recv()
+
+            @pl.when(unit == BASE[pair])
+            def _():
+                for step in (LOCAL + 2 * pair, LOCAL + 2 * pair + 1):
+                    forward(step).wait_recv()
+
+        process(recv.at[unit], result.at[unit])
+
+        @pl.when(unit == OWN)
+        def _():
+            relay()
+
+        for step in range(1, LOCAL):
+            @pl.when(unit == NEAR[step])
+            def _():
+                returning(step).start()
+
+        for pair in range(2):
+            @pl.when(unit == OVER[pair])
+            def _():
+                for step in range(max(1, 2 * pair), 2 * pair + 2):
+                    fan_home(step).start()
+
+            @pl.when(unit == BASE[pair])
+            def _():
+                for step in (LOCAL + 2 * pair, LOCAL + 2 * pair + 1):
+                    returning(step).start()
+
+        @pl.when(unit == BASE[1])
+        def _():
+            collect()
+
+    @pl.loop(EARLY, text_blocks)
+    def _(block):
+        text(block)
+
+    sought = jnp.broadcast_to(target, (rows, rows)).T
+    lane = lax.broadcasted_iota(jnp.int32, (rows, rows), 1).astype(jnp.float32)
+    local_rows = LOCAL * held * BLOCK
+    cross_rows = places - local_rows
+    from_near = one_hot(sought == lane)
+    from_far = one_hot(sought == lane + float(local_rows))[:, :cross_rows]
+
+    for turn in range(1, replicas):
+        tell(turn).wait()
+    full = jnp.max(group_send[...].astype(jnp.float32))
+    for turn in range(1, replicas):
+        full = jnp.maximum(full, jnp.max(group_recv[turn - 1].astype(jnp.float32)))
+    flag_ref[0] = full.astype(jnp.int32)
+
+    @pl.loop(1, devices)
+    def _(step):
+        meta(step).wait_send()
+
+    bundle_out().wait_send()
+    for step in range(1, LOCAL):
+        fan_out(step).wait_send()
+        fan_home(step).wait_send()
+    bundle_home().wait()
+    for step in range(1, devices):
+        forward(step).wait_send()
+        returning(step).wait()
+
+    def block_of(number, rows_of):
+        return (result if number == OWN else back)[number, rows_of]
+
+    planes = jnp.stack([block_of(number, held * local_heads) for number in BLOCKS], axis=0)
+    spread = spread_planes(planes, held)
+    parts = jnp.dot(from_near, spread[:local_rows], preferred_element_type=jnp.float32)
+    parts = parts + jnp.dot(
+        from_far,
+        jnp.concatenate([spread[local_rows:], bundle_back[local_heads]], axis=0),
+        preferred_element_type=jnp.float32,
+    )
+    image_lse = parts
+    for piece in range(1, SPLIT * held):
+        image_lse = image_lse + pltpu.roll(parts, head_size - LANES * piece, 1)
+    own_lse = text_lse[...]
+    upper = jnp.maximum(image_lse, own_lse)
+    image_weight = jnp.exp(image_lse - upper)
+    text_weight = jnp.exp(own_lse - upper)
+    whole = image_weight + text_weight
+    image_weight = image_weight / whole
+    text_weight = text_weight / whole
+
+    for head in range(local_heads):
+        pieces = [
+            block_of(number, which * local_heads + head)
+            for number in BLOCKS
+            for which in range(held)
+        ]
+        middle = LOCAL * held
+        image_part = jnp.dot(
+            from_near,
+            jnp.concatenate(pieces[:middle], axis=0),
+            preferred_element_type=jnp.float32,
+        ) + jnp.dot(
+            from_far,
+            jnp.concatenate(pieces[middle:] + [bundle_back[head]], axis=0),
+            preferred_element_type=jnp.float32,
+        )
+        merged = (
+            image_weight[:, head : head + 1] * image_part
+            + text_weight[:, head : head + 1] * text_out[head]
+        )
+        out_ref[head] = merged.astype(jnp.bfloat16)
+
+
 def on_device(
     queries,
     request_image,
@@ -337,53 +881,100 @@
     devices = lax.axis_size("seq")
     most = -(-max(2, 2 * rows // images) // BLOCK) * BLOCK
     hbm = pl.BlockSpec(memory_space=pltpu.HBM)
-    moved = pl.pallas_call(
-        functools.partial(kernel, devices, held, most, group),
-        out_shape=pltpu.VMEM((local_heads, rows, head_size), jnp.bfloat16),
+    operands = [
+        pltpu.with_memory_space_constraint(operand, pltpu.HBM)
+        for operand in (
+            image_slot,
+            image_lengths,
+            request_image.reshape(1, rows),
+            text_lengths.reshape(1, rows),
+            jnp.transpose(queries, (1, 0, 2)),
+            image_keys,
+            image_values,
+            text_keys,
+            text_values,
+        )
+    ]
+    outcome = pltpu.VMEM((local_heads, rows, head_size), jnp.bfloat16)
+    common = [
+        pltpu.SMEM(image_slot.shape, jnp.int32),
+        pltpu.SMEM(image_lengths.shape, jnp.int32),
+        pltpu.VMEM((1, rows), jnp.int32),
+        pltpu.VMEM((1, rows), jnp.int32),
+        pltpu.VMEM((local_heads, rows, head_size), jnp.bfloat16),
+        pltpu.VMEM(image_keys.shape, jnp.bfloat16),
+        pltpu.VMEM(image_values.shape, jnp.bfloat16),
+        pltpu.VMEM(text_keys.shape, jnp.bfloat16),
+        pltpu.VMEM(text_values.shape, jnp.bfloat16),
+    ]
+    texts = [
+        pltpu.VMEM((local_heads, rows, head_size), jnp.float32),
+        pltpu.VMEM((rows, head_size), jnp.float32),
+        pltpu.VMEM((rows, rows), jnp.float32),
+        pltpu.SemaphoreType.DMA((9,)),
+    ]
+    results = held * local_heads + 1
+
+    def plain(identity):
+        return pl.pallas_call(
+            functools.partial(kernel, devices, held, most, group),
+            out_shape=outcome,
+            in_specs=[hbm] * 9,
+            out_specs=pl.BlockSpec(memory_space=pltpu.VMEM),
+            scratch_shapes=common
+            + [
+                pltpu.VMEM((devices, held, local_heads, most, head_size), jnp.bfloat16),
+                pltpu.VMEM((devices, held, local_heads, most, head_size), jnp.bfloat16),
+                pltpu.VMEM((devices, results, most, head_size), jnp.bfloat16),
+                pltpu.VMEM((devices, results, most, head_size), jnp.bfloat16),
+            ]
+            + texts
+            + [pltpu.SemaphoreType.DMA((devices,))] * 4,
+            compiler_params=pltpu.CompilerParams(
+                collective_id=identity, has_side_effects=True, vmem_limit_bytes=LIMIT
+            ),
+        )(*operands)
+
+    if devices != 2 * LOCAL or most != BLOCK or 2 * rows // images <= BLOCK // 2:
+        return jnp.transpose(plain(0), (1, 0, 2))
+
+    replicas = lax.axis_size("groups")
+    spare = rows // 4
+    half = BLOCK // 2
+    moved, flag = pl.pallas_call(
+        functools.partial(fast_kernel, devices, replicas, held, group, spare),
+        out_shape=(outcome, pltpu.SMEM((1,), jnp.int32)),
         in_specs=[hbm] * 9,
-        out_specs=pl.BlockSpec(memory_space=pltpu.VMEM),
-        scratch_shapes=[
-            pltpu.SMEM(image_slot.shape, jnp.int32),
-            pltpu.SMEM(image_lengths.shape, jnp.int32),
+        out_specs=(
+            pl.BlockSpec(memory_space=pltpu.VMEM),
+            pl.BlockSpec(memory_space=pltpu.SMEM),
+        ),
+        scratch_shapes=common
+        + [
+            pltpu.VMEM((LOCAL + 1, held, local_heads, BLOCK, head_size), jnp.bfloat16),
+            pltpu.VMEM((UNITS, held, local_heads, BLOCK, head_size), jnp.bfloat16),
+            pltpu.VMEM((UNITS, results, BLOCK, head_size), jnp.bfloat16),
+            pltpu.VMEM((UNITS, results, BLOCK, head_size), jnp.bfloat16),
+            pltpu.VMEM((2, held, local_heads, BLOCK, head_size), jnp.bfloat16),
+            pltpu.VMEM((2, results, BLOCK, head_size), jnp.bfloat16),
+            pltpu.VMEM((local_heads, spare, head_size), jnp.bfloat16),
+            pltpu.VMEM((local_heads, spare, head_size), jnp.bfloat16),
+            pltpu.VMEM((local_heads + 1, spare, head_size), jnp.bfloat16),
+            pltpu.VMEM((local_heads + 1, spare, head_size), jnp.bfloat16),
+            pltpu.VMEM((devices, 1, rows), jnp.int32),
             pltpu.VMEM((1, rows), jnp.int32),
-            pltpu.VMEM((1, rows), jnp.int32),
-            pltpu.VMEM((local_heads, rows, head_size), jnp.bfloat16),
-            pltpu.VMEM(image_keys.shape, jnp.bfloat16),
-            pltpu.VMEM(image_values.shape, jnp.bfloat16),
-            pltpu.VMEM(text_keys.shape, jnp.bfloat16),
-            pltpu.VMEM(text_values.shape, jnp.bfloat16),
-            pltpu.VMEM((devices, held, local_heads, most, head_size), jnp.bfloat16),
-            pltpu.VMEM((devices, held, local_heads, most, head_size), jnp.bfloat16),
-            pltpu.VMEM((devices, held * local_heads + 1, most, head_size), jnp.bfloat16),
-            pltpu.VMEM((devices, held * local_heads + 1, most, head_size), jnp.bfloat16),
-            pltpu.VMEM((local_heads, rows, head_size), jnp.float32),
-            pltpu.VMEM((rows, head_size), jnp.float32),
-            pltpu.VMEM((rows, rows), jnp.float32),
-            pltpu.SemaphoreType.DMA((9,)),
-            pltpu.SemaphoreType.DMA((devices,)),
-            pltpu.SemaphoreType.DMA((devices,)),
-            pltpu.SemaphoreType.DMA((devices,)),
-            pltpu.SemaphoreType.DMA((devices,)),
-        ],
+            pltpu.VMEM((max(1, replicas - 1), 1, rows), jnp.int32),
+        ]
+        + texts
+        + [pltpu.SemaphoreType.DMA((devices,))] * 4
+        + [pltpu.SemaphoreType.DMA((LOCAL,))] * 5
+        + [pltpu.SemaphoreType.DMA((devices,))] * 2
+        + [pltpu.SemaphoreType.DMA((max(1, replicas - 1),))] * 2,
         compiler_params=pltpu.CompilerParams(
             collective_id=0, has_side_effects=True, vmem_limit_bytes=LIMIT
         ),
-    )(
-        *(
-            pltpu.with_memory_space_constraint(operand, pltpu.HBM)
-            for operand in (
-                image_slot,
-                image_lengths,
-                request_image.reshape(1, rows),
-                text_lengths.reshape(1, rows),
-                jnp.transpose(queries, (1, 0, 2)),
-                image_keys,
-                image_values,
-                text_keys,
-                text_values,
-            )
-        )
-    )
+    )(*operands)
+    moved = lax.cond(flag[0] > 0, lambda: plain(1), lambda: moved)
     return jnp.transpose(moved, (1, 0, 2))
 
 

time: 47.2 us -> 42.5 us (0.900)
  the two profiles are of different devices: /device:TPU:10 before, /device:TPU:0 now
where the time goes in v2:
time: 42.5 us; the launch traced here: 42.4 us
  Pallas kernels  41.6 us (98%)
  local copies, waits for them, and re-layouts  0.77 us (2%)
    pallas_call x1, Pallas kernels, on_device(): pl.pallas_call(functools.partial(fast_kernel, devices, replicas, held, gr...  41.6 us

profile of v2, /device:TPU:0, one launch (start us, length us, event | category | flops | bytes accessed | tf_op | source)
XLA Modules:
  0.0 42.4 jit_solution(4438340679484395805)
XLA Ops:
  0.0 41.6 %shard_map.91 = (bf16[14,128,128]{2,1,0:T(8,128)(2,1)S(1)}, s32[1]{0:T(128)S(4)}) custom-call(s32[16]{0:T(128)} %slot_hbm.1, s32[2]{0:T(128)} %length_hbm.1, s32[1,128]{1,0:T(1,128)} %bitcast.8, s32[1,128]{1,0:T(1,128)} %bitcast.10, bf16[14,128,128]{2,1,0:T(8,128)(2,1)} %bitcast.6, bf16[2,2,1280,128]{3,2,1,0:T(8,128)(2,1)} %ikey_hbm.1, ...), custom_call_target="tpu_custom_call" | custom-call | tf_op jit(solution)/shard_map/pallas_call | solution.py:944
  41.6 0.8 %copy.13 = bf16[128,14,128]{2,0,1:T(8,128)(2,1)} copy(bf16[128,14,128]{2,0,1:T(8,128)(2,1)S(1)} %bitcast.5) | data formatting | bytes 917504
  (1 shorter events, 0.0 us)
